TPU v7x, 32 devices: a whole 2x2x4 slice. The times are simulated.
32 devices in a mesh: ctx: 16 (over z, x, core), fsdp: 2 (over y).
Axes of the slice: x: 2, y: 2, z: 4, core: 2. Of those that a mesh axis runs over, the one named last changes fastest.
Arguments:
- tokens: bfloat16 [2, 2048, 1024], P('fsdp', 'ctx'), may hold values from -6 to 6
- cotangent: bfloat16 [2, 2048, 1024], P('fsdp', 'ctx'), may hold values from -6 to 6
- gain_attn: float32 [1024], replicated, may hold values from 0.5 to 1.5
- gain_mlp: float32 [1024], replicated, may hold values from 0.5 to 1.5
- qkv_weight: bfloat16 [3072, 1024], P('fsdp'), may hold values from -2 to 2
- out_weight: bfloat16 [1024, 1024], P('fsdp'), may hold values from -0.625 to 0.625
- in_weight: bfloat16 [5248, 1024], P('fsdp'), may hold values from -0.1875 to 0.1875
- down_weight: bfloat16 [1024, 2624], P('fsdp'), may hold values from -0.125 to 0.125
Outputs:
- output: float32 [2, 2048, 1024], P('fsdp', 'ctx')
- grad_input: float32 [2, 2048, 1024], P('fsdp', 'ctx')
- grad_qkv: float32 [3072, 1024], P(('ctx', 'fsdp'))
- grad_out_proj: float32 [1024, 1024], P(('ctx', 'fsdp'))
- grad_in_proj: float32 [5248, 1024], P(('ctx', 'fsdp'))
- grad_down: float32 [1024, 2624], P(('ctx', 'fsdp'))
- grad_gain_attn: float32 [1024], P(('ctx', 'fsdp'))
- grad_gain_mlp: float32 [1024], P(('ctx', 'fsdp'))
All inputs are finite; a program needn't handle non-finite values.
Results may differ from a plain program's by a relative error of at most 0.015.
Values may be sent and summed in bfloat16 or wider, within the bound.
A program may use at most 256 MiB of HBM per device.

v0:
```python
import math
import jax
import jax.numpy as jnp
from jax import lax
from jax.sharding import PartitionSpec as P

HEAD_DIM = 64
EPSILON = 1e-05
ROPE_BASE = 160000.0


def normalize(tensor):
    centred = tensor - jnp.mean(tensor, axis=-1, keepdims=True)
    inv_std = lax.rsqrt(jnp.mean(centred * centred, axis=-1, keepdims=True) + EPSILON)
    return (centred * inv_std, inv_std)


def norm_back(grad_norm, normed, inv_std):
    return inv_std * (
        grad_norm
        - jnp.mean(grad_norm, axis=-1, keepdims=True)
        - normed * jnp.mean(grad_norm * normed, axis=-1, keepdims=True)
    )


def gelu_pair(tensor):
    cumul = 0.5 * (1.0 + jax.scipy.special.erf(tensor * 0.7071067811865476))
    density = jnp.exp(-0.5 * tensor * tensor) * 0.3989422804014327
    return (tensor * cumul, cumul + tensor * density)


def rope_tables(offset, length, head_size):
    positions = (offset + jnp.arange(length, dtype=jnp.int32)).astype(jnp.float32)
    inverse = ROPE_BASE ** (
        -jnp.arange(0, head_size, 2, dtype=jnp.int32).astype(jnp.float32) / head_size
    )
    angles = positions[:, None] * inverse[None, :]
    angles = jnp.concatenate([angles, angles], axis=-1)
    return (jnp.cos(angles)[:, None, :], jnp.sin(angles)[:, None, :])


def rotate(tensor, cos_table, sine_table):
    middle = tensor.shape[-1] // 2
    turned = jnp.concatenate([-tensor[..., middle:], tensor[..., :middle]], axis=-1)
    return tensor * cos_table + turned * sine_table


def rotate_back(gradient, cos_table, sine_table):
    middle = gradient.shape[-1] // 2
    scaled = gradient * sine_table
    turned = jnp.concatenate([scaled[..., middle:], -scaled[..., :middle]], axis=-1)
    return gradient * cos_table + turned


def rows_product(left, right):
    return lax.dot_general(
        left, right, (((1,), (1,)), ((), ())), preferred_element_type=jnp.float32
    )


def rows_contract(left, right):
    return lax.dot_general(
        left, right, (((0,), (0,)), ((), ())), preferred_element_type=jnp.float32
    )


def per_device(
    tokens, cotangent, gain_attn, gain_mlp, qkv_weight, out_weight, in_weight, down_weight
):
    f32 = jnp.float32
    bf16 = jnp.bfloat16
    qkv_full, out_full, in_full, down_full = (
        lax.all_gather(qkv_weight, "fsdp", axis=0, tiled=True),
        lax.all_gather(out_weight, "fsdp", axis=0, tiled=True),
        lax.all_gather(in_weight, "fsdp", axis=0, tiled=True),
        lax.all_gather(down_weight, "fsdp", axis=0, tiled=True),
    )
    tok_rows = tokens.shape[1]
    width = tokens.shape[2]
    hidden = down_full.shape[1]
    head_size = HEAD_DIM
    head_count = width // head_size
    scale = head_size ** (-0.5)
    offset = lax.axis_index("ctx") * tok_rows
    cos_table, sine_table = rope_tables(offset, tok_rows, head_size)
    resid = tokens[0].astype(f32)
    normed_a, inv_a = normalize(resid)
    act_a = (normed_a * gain_attn).astype(bf16)
    packed = rows_product(act_a, qkv_full)
    query_heads = rotate(
        packed[:, :width].reshape(tok_rows, head_count, head_size), cos_table, sine_table
    ).astype(bf16)
    key_heads = rotate(
        packed[:, width : 2 * width].reshape(tok_rows, head_count, head_size), cos_table, sine_table
    ).astype(bf16)
    value_send = packed[:, 2 * width :].astype(bf16)
    key_send = key_heads.reshape(tok_rows, width)
    value_heads = value_send.reshape(tok_rows, head_count, head_size)
    start_state = (
        jnp.zeros((tok_rows, head_count, head_size), f32),
        jnp.full((head_count, tok_rows), -1e30, f32),
        jnp.zeros((head_count, tok_rows), f32),
    )
    key_piece = lax.all_gather(key_send, "ctx", axis=0, tiled=True)
    value_piece = lax.all_gather(value_send, "ctx", axis=0, tiled=True)
    length = key_piece.shape[0]
    step_len = math.gcd(length, 1024)

    def attend_block(block_num, running):
        weighted, row_max, row_sum = running
        key_blk = lax.dynamic_slice_in_dim(key_piece, block_num * step_len, step_len, 0).reshape(
            step_len, head_count, head_size
        )
        value_blk = lax.dynamic_slice_in_dim(
            value_piece, block_num * step_len, step_len, 0
        ).reshape(step_len, head_count, head_size)
        scores = (
            jnp.einsum("qhd,khd->hqk", query_heads, key_blk, preferred_element_type=f32) * scale
        )
        new_max = jnp.maximum(row_max, jnp.max(scores, axis=-1))
        shrink = jnp.exp(row_max - new_max)
        weights = jnp.exp(scores - new_max[..., None])
        row_sum = row_sum * shrink + jnp.sum(weights, axis=-1)
        weighted = weighted * shrink.T[:, :, None] + jnp.einsum(
            "hqk,khd->qhd", weights.astype(bf16), value_blk, preferred_element_type=f32
        )
        return (weighted, new_max, row_sum)

    weighted, row_max, row_sum = lax.fori_loop(0, length // step_len, attend_block, start_state)
    log_sum = row_max + jnp.log(row_sum)
    mixed = (weighted / row_sum.T[:, :, None]).reshape(tok_rows, width).astype(bf16)
    middle = resid + rows_product(mixed, out_full)
    normed_m, inv_m = normalize(middle)
    act_m = (normed_m * gain_mlp).astype(bf16)
    inner = rows_product(act_m, in_full)
    gelu_val, gelu_slope = gelu_pair(inner[:, :hidden])
    gated = (gelu_val * inner[:, hidden:]).astype(bf16)
    output = middle + rows_product(gated, down_full)
    cot_rows = cotangent[0]
    grad_down = rows_contract(cot_rows, gated)
    grad_gated = jnp.dot(cot_rows, down_full, preferred_element_type=f32)
    grad_inner = jnp.concatenate(
        [grad_gated * inner[:, hidden:] * gelu_slope, grad_gated * gelu_val], axis=1
    ).astype(bf16)
    grad_in = rows_contract(grad_inner, act_m)
    grad_act_m = jnp.dot(grad_inner, in_full, preferred_element_type=f32)
    grad_gain_m = jnp.sum(grad_act_m * normed_m, axis=0)
    grad_middle = cot_rows.astype(f32) + norm_back(grad_act_m * gain_mlp, normed_m, inv_m)
    grad_mid_bf = grad_middle.astype(bf16)
    grad_out = rows_contract(grad_mid_bf, mixed)
    grad_mixed = jnp.dot(grad_mid_bf, out_full, preferred_element_type=f32).astype(bf16)
    grad_heads = grad_mixed.reshape(tok_rows, head_count, head_size)
    delta_rows = jnp.sum(
        grad_heads.astype(f32) * mixed.reshape(tok_rows, head_count, head_size).astype(f32), axis=-1
    )
    delta = delta_rows.T
    zeros_heads = jnp.zeros((tok_rows, head_count, head_size), f32)
    query_key_piece = lax.all_gather(key_send, "ctx", axis=0, tiled=True)
    query_value_piece = lax.all_gather(value_send, "ctx", axis=0, tiled=True)
    length = query_key_piece.shape[0]
    query_step_len = math.gcd(length, 1024)

    def query_grad_block(block_num, grad_query):
        key_blk = lax.dynamic_slice_in_dim(
            query_key_piece, block_num * query_step_len, query_step_len, 0
        ).reshape(query_step_len, head_count, head_size)
        value_blk = lax.dynamic_slice_in_dim(
            query_value_piece, block_num * query_step_len, query_step_len, 0
        ).reshape(query_step_len, head_count, head_size)
        scores = (
            jnp.einsum("qhd,khd->hqk", query_heads, key_blk, preferred_element_type=f32) * scale
        )
        probs = jnp.exp(scores - log_sum[..., None])
        grad_probs = jnp.einsum("qhd,khd->hqk", grad_heads, value_blk, preferred_element_type=f32)
        grad_scores = (probs * (grad_probs - delta[..., None])).astype(bf16)
        return (
            grad_query
            + jnp.einsum("hqk,khd->qhd", grad_scores, key_blk, preferred_element_type=f32) * scale
        )

    grad_query = lax.fori_loop(0, length // query_step_len, query_grad_block, zeros_heads)
    query_send = query_heads.reshape(tok_rows, width).astype(f32)
    grad_send = grad_mixed.astype(f32)
    query_piece = lax.all_gather(query_send, "ctx", axis=0, tiled=True)
    grad_piece = lax.all_gather(grad_send, "ctx", axis=0, tiled=True)
    log_piece = lax.all_gather(log_sum.T, "ctx", axis=0, tiled=True)
    delta_piece = lax.all_gather(delta_rows, "ctx", axis=0, tiled=True)
    length = query_piece.shape[0]
    key_step_len = math.gcd(length, 1024)

    def key_grad_block(block_num, running):
        grad_keys, grad_values = running
        query_blk = (
            lax.dynamic_slice_in_dim(query_piece, block_num * key_step_len, key_step_len, 0)
            .astype(bf16)
            .reshape(key_step_len, head_count, head_size)
        )
        grad_blk = (
            lax.dynamic_slice_in_dim(grad_piece, block_num * key_step_len, key_step_len, 0)
            .astype(bf16)
            .reshape(key_step_len, head_count, head_size)
        )
        log_blk = lax.dynamic_slice_in_dim(log_piece, block_num * key_step_len, key_step_len, 0).T
        delta_blk = lax.dynamic_slice_in_dim(
            delta_piece, block_num * key_step_len, key_step_len, 0
        ).T
        scores = (
            jnp.einsum("qhd,khd->hqk", query_blk, key_heads, preferred_element_type=f32) * scale
        )
        probs = jnp.exp(scores - log_blk[..., None])
        grad_values = grad_values + jnp.einsum(
            "hqk,qhd->khd", probs.astype(bf16), grad_blk, preferred_element_type=f32
        )
        grad_probs = jnp.einsum("qhd,khd->hqk", grad_blk, value_heads, preferred_element_type=f32)
        grad_scores = (probs * (grad_probs - delta_blk[..., None])).astype(bf16)
        grad_keys = (
            grad_keys
            + jnp.einsum("hqk,qhd->khd", grad_scores, query_blk, preferred_element_type=f32) * scale
        )
        return (grad_keys, grad_values)

    grad_keys, grad_values = lax.fori_loop(
        0, length // key_step_len, key_grad_block, (zeros_heads, zeros_heads)
    )
    grad_query = rotate_back(grad_query, cos_table, sine_table)
    grad_keys = rotate_back(grad_keys, cos_table, sine_table)
    grad_packed = jnp.concatenate(
        [
            grad_query.reshape(tok_rows, width),
            grad_keys.reshape(tok_rows, width),
            grad_values.reshape(tok_rows, width),
        ],
        axis=1,
    ).astype(bf16)
    grad_qkv = rows_contract(grad_packed, act_a)
    grad_act_a = jnp.dot(grad_packed, qkv_full, preferred_element_type=f32)
    grad_gain_a = jnp.sum(grad_act_a * normed_a, axis=0)
    grad_input = grad_middle + norm_back(grad_act_a * gain_attn, normed_a, inv_a)
    owned = (
        lax.psum_scatter(grad_qkv, ("ctx", "fsdp"), scatter_dimension=0, tiled=True),
        lax.psum_scatter(grad_out, ("ctx", "fsdp"), scatter_dimension=0, tiled=True),
        lax.psum_scatter(grad_in, ("ctx", "fsdp"), scatter_dimension=0, tiled=True),
        lax.psum_scatter(grad_down, ("ctx", "fsdp"), scatter_dimension=0, tiled=True),
        lax.psum_scatter(grad_gain_a, ("ctx", "fsdp"), scatter_dimension=0, tiled=True),
        lax.psum_scatter(grad_gain_m, ("ctx", "fsdp"), scatter_dimension=0, tiled=True),
    )
    return (
        output[None],
        grad_input[None],
        owned[0],
        owned[1],
        owned[2],
        owned[3],
        owned[4],
        owned[5],
    )


def solution(mesh):
    return jax.shard_map(
        per_device,
        mesh=mesh,
        in_specs=(
            P("fsdp", "ctx", None),
            P("fsdp", "ctx", None),
            P(),
            P(),
            P("fsdp", None),
            P("fsdp", None),
            P("fsdp", None),
            P("fsdp", None),
        ),
        out_specs=(
            P("fsdp", "ctx", None),
            P("fsdp", "ctx", None),
            P(("ctx", "fsdp"), None),
            P(("ctx", "fsdp"), None),
            P(("ctx", "fsdp"), None),
            P(("ctx", "fsdp"), None),
            P(("ctx", "fsdp")),
            P(("ctx", "fsdp")),
        ),
        check_vma=False,
    )
```

profile of v0, /device:TPU:14, one launch (start us, length us, event | category | flops | bytes accessed | tf_op | source)
XLA Modules:
  0.0 1275.8 jit_solution(7228493947482920155)
XLA Ops:
  9.6 80.5 %all-gather.9.cloned.1.call-done = bf16[3072,1024]{1,0:T(8,128)(2,1)} async-done(((bf16[1536,1024]{1,0:T(8,128)(2,1)}), bf16[3072,1024]{1,0:T(8,128)(2,1)}) %all-gather.9.cloned.1.call-update) | async-done | bytes 6291472 | tf_op jit(solution)/shard_map/all_gather | solution.py:73
  90.1 5.0 fusion.85
  106.7 47.2 %all-gather.11.cloned.1.call-done = bf16[2048,1024]{1,0:T(8,128)(2,1)} async-done(((bf16[128,1024]{1,0:T(8,128)(2,1)}), bf16[2048,1024]{1,0:T(8,128)(2,1)}) %all-gather.11.cloned.1.call-update) | async-done | bytes 4194320 | tf_op jit(solution)/shard_map/all_gather | solution.py:104
  153.9 6.5 copy.63
  160.4 44.6 %all-gather.13.cloned.1.call-done = bf16[2048,1024]{1,0:T(8,128)(2,1)} async-done(((bf16[128,1024]{1,0:T(8,128)(2,1)}), bf16[2048,1024]{1,0:T(8,128)(2,1)}) %all-gather.13.cloned.1.call-update) | async-done | bytes 4194320 | tf_op jit(solution)/shard_map/all_gather | solution.py:105
  205.0 6.5 copy.64
  211.5 29.9 %while.48 = (s32[]{:T(128)}, f32[128,16,64]{0,2,1:T(8,128)S(1)}, f32[16,128]{1,0:T(8,128)S(1)}, f32[16,128]{1,0:T(8,128)S(1)}, bf16[2048,1024]{0,1:T(8,128)(2,1)...) while((s32[]{:T(128)}, f32[128,16,64]{0,2,1:T(8,128)S(1)}, ...), condition=%wide.region_5.0_spmd.clone, body=%wide.region_2.0_spmd.clone.sunk | while | flops 554053632 | bytes 72745168 | solution.py:129
  214.6 4.8 bitcast_reduce_fusion.2
  219.4 5.3 fusion.148
  234.1 5.3 fusion.148
  244.3 127.5 %all-gather.17.cloned.1.call-done = bf16[5248,1024]{1,0:T(8,128)(2,1)} async-done(((bf16[2624,1024]{1,0:T(8,128)(2,1)}), bf16[5248,1024]{1,0:T(8,128)(2,1)}) %all-gather.17.cloned.1.call-update) | async-done | bytes 10747920 | tf_op jit(solution)/shard_map/all_gather | solution.py:75
  371.8 9.3 fusion.87
  381.1 62.2 %all-gather.19.cloned.1.call-done = bf16[1024,2624]{0,1:T(8,128)(2,1)} async-done(((bf16[512,2624]{0,1:T(8,128)(2,1)}), bf16[1024,2624]{0,1:T(8,128)(2,1)}) %all-gather.19.cloned.1.call-update) | async-done | bytes 5373968 | tf_op jit(solution)/shard_map/all_gather | solution.py:76
  443.3 5.3 fusion.48
  448.6 7.1 multiply_reduce_fusion
  460.0 7.7 convolution_bitcast_fusion
  467.7 12.1 copy.78
  483.0 15.4 %all_gather.39 = f32[2048,16]{0,1:T(8,128)S(1)} all-gather(f32[128,16]{0,1:T(8,128)S(1)} %bitcast.218), channel_id=1, replica_groups=mesh['ctx'=16,'fsdp'=2] {'ctx'}, dimensions={0}, use_global_device_ids=true | all-gather | bytes 139264 | tf_op jit(solution)/shard_map/all_gather | solution.py:186
  499.5 22.1 %all_gather.41 = f32[2048,16]{0,1:T(8,128)S(1)} all-gather(f32[128,16]{0,1:T(8,128)S(1)} %multiply_reduce_fusion.1), channel_id=1, replica_groups=mesh['ctx'=16,'fsdp'=2] {'ctx'}, dimensions={0}, use_global_device_ids=true | all-gather | bytes 139264 | tf_op jit(solution)/shard_map/all_gather | solution.py:187
  521.6 33.4 %while.49 = (s32[]{:T(128)}, f32[128,16,64]{0,2,1:T(8,128)}, bf16[2048,1024]{0,1:T(8,128)(2,1)}, bf16[128,16,64]{0,2,1:T(8,128)(2,1)S(1)}, f32[16,128]{1,0:T(8,1...) while((s32[]{:T(128)}, f32[128,16,64]{0,2,1:T(8,128)}, ...), condition=%wide.region_12.0_spmd.clone, body=%wide.region_11.0_spmd.clone.sunk | while | flops 816185344 | bytes 33079508 | solution.py:181
  530.2 8.1 fusion.157
  546.9 8.0 fusion.157
  555.0 65.2 %while.50 = (s32[]{:T(128)}, f32[128,16,64]{0,2,1:T(8,128)}, f32[128,16,64]{0,2,1:T(8,128)S(1)}, bf16[2048,1024]{1,0:T(8,128)(2,1)}, bf16[128,16,64]{0,2,1:T(8,1...) while((s32[]{:T(128)}, f32[128,16,64]{0,2,1:T(8,128)}, ...), condition=%wide.region_14.0_spmd.clone, body=%wide.region_13.0_spmd.clone.sunk | while | flops 1091174400 | bytes 53412036 | solution.py:222
  571.4 10.8 fusion.166
  582.2 5.5 fusion.167
  603.9 10.8 fusion.166
  614.7 5.5 fusion.167
  622.9 6.4 fusion.69
  630.8 9.2 fusion.50
  640.0 547.2 %fusion = f32[168,1024]{1,0:T(8,128)} fusion(f32[5248,1024]{1,0:T(8,128)} %fusion.50), kind=kCustom, calls=%all-reduce-scatter | all-reduce-scatter fusion | flops 5505025 | bytes 22183936
  1197.4 8.4 collective-permute-done
  1213.9 52.7 %all-reduce.4 = (f32[1024]{0:T(1024)S(1)}, f32[1024]{0:T(1024)S(1)}) all-reduce(f32[1024]{0:T(1024)S(1)} %get-tuple-element.613, f32[1024]{0:T(1024)S(1)} %copy-done.43), channel_id=6, replica_groups=mesh['ctx'=16,'fsdp'=2] {'ctx','fsdp'}, use_global_device_ids=true, to_apply=%region_22.0.clone | all-reduce | flops 2048 | bytes 16384
  (200 shorter events, 113.4 us)
Async XLA Ops:
  7.2 82.9 %copy-start.29 = (f32[1024]{0:T(1024)S(1)}, f32[1024]{0:T(1024)}, u32[]{:S(2)}) copy-start(f32[1024]{0:T(1024)} %param.16) | copy-start | bytes 12292
  7.2 82.9 %all-gather.9.cloned.1.call-start = ((), (), s32[]{:S(2)}) async-start(), calls=%async_computation.3 | async-start | bytes 9437184 | tf_op jit(solution)/shard_map/all_gather | solution.py:73
  7.9 146.0 %all-gather.11.cloned.1.call-start = ((), (), s32[]{:S(2)}) async-start(), calls=%async_computation.4 | async-start | bytes 4456448 | tf_op jit(solution)/shard_map/all_gather | solution.py:104
  8.2 89.4 %copy-start.25 = (f32[128,64]{0,1:T(8,128)}, f32[128,64]{0,1:T(8,128)S(1)}, u32[]{:S(2)}) copy-start(f32[128,64]{0,1:T(8,128)S(1)} %get-tuple-element.704) | copy-start | bytes 98308
  8.2 89.4 %copy-start.27 = (f32[128,64]{0,1:T(8,128)}, f32[128,64]{0,1:T(8,128)S(1)}, u32[]{:S(2)}) copy-start(f32[128,64]{0,1:T(8,128)S(1)} %get-tuple-element.703) | copy-start | bytes 98308
  9.3 85.8 %copy-start.35 = (f32[128]{0:T(128)}, f32[128]{0:T(128)S(1)}, u32[]{:S(2)}) copy-start(f32[128]{0:T(128)S(1)} %broadcast_multiply_fusion.8) | copy-start | bytes 1540
  9.6 85.5 %copy-start.37 = (f32[128]{0:T(128)}, f32[128]{0:T(128)S(1)}, u32[]{:S(2)}) copy-start(f32[128]{0:T(128)S(1)} %add_rsqrt_fusion.1) | copy-start | bytes 1540
  103.3 101.7 %all-gather.13.cloned.1.call-start = ((), (), s32[]{:S(2)}) async-start(), calls=%async_computation.5 | async-start | bytes 4456448 | tf_op jit(solution)/shard_map/all_gather | solution.py:105
  104.1 137.4 %all-gather.15.cloned.1.call-start = ((), (), s32[]{:S(2)}) async-start(), calls=%async_computation.6 | async-start | bytes 3145728 | tf_op jit(solution)/shard_map/all_gather | solution.py:74
  104.7 267.1 %all-gather.17.cloned.1.call-start = ((), (), s32[]{:S(2)}) async-start(), calls=%async_computation.7 | async-start | bytes 16121856 | tf_op jit(solution)/shard_map/all_gather | solution.py:75
  105.3 338.0 %all-gather.19.cloned.1.call-start = ((), (), s32[]{:S(2)}) async-start(), calls=%async_computation.8 | async-start | bytes 8060928 | tf_op jit(solution)/shard_map/all_gather | solution.py:76
  105.9 449.1 %all-gather.21.cloned.1.call-start = ((), (), s32[]{:S(2)}) async-start(), calls=%async_computation.9 | async-start | bytes 4456448 | tf_op jit(solution)/shard_map/all_gather | solution.py:184
  106.6 448.3 %all-gather.23.cloned.1.call-start = ((), (), s32[]{:S(2)}) async-start(), calls=%async_computation.10 | async-start | bytes 4456448 | tf_op jit(solution)/shard_map/all_gather | solution.py:185
  241.4 130.4 %copy-start.31 = (f32[1024]{0:T(1024)S(1)}, f32[1024]{0:T(1024)}, u32[]{:S(2)}) copy-start(f32[1024]{0:T(1024)} %param.17) | copy-start | bytes 12292
  244.0 211.6 %copy-start.1 = (f32[128,1024]{1,0:T(8,128)}, f32[128,1024]{1,0:T(8,128)S(1)}, u32[]{:S(2)}) copy-start(f32[128,1024]{1,0:T(8,128)S(1)} %get-tuple-element.706) | copy-start | bytes 1572868
  244.1 211.6 %copy-start.39 = (f32[128]{0:T(128)}, f32[128]{0:T(128)S(1)}, u32[]{:S(2)}) copy-start(f32[128]{0:T(128)S(1)} %broadcast_multiply_fusion.7) | copy-start | bytes 1540
  244.3 211.4 %copy-start.41 = (f32[128]{0:T(128)}, f32[128]{0:T(128)S(1)}, u32[]{:S(2)}) copy-start(f32[128]{0:T(128)S(1)} %add_rsqrt_fusion) | copy-start | bytes 1540
  244.3 199.0 %copy-start.20 = (bf16[1,128,1024]{2,1,0:T(8,128)(2,1)S(1)}, bf16[1,128,1024]{2,1,0:T(8,128)(2,1)}, u32[]{:S(2)}) copy-start(bf16[1,128,1024]{2,1,0:T(8,128)(2,1)} %param.15) | copy-start | bytes 786436
  448.5 7.1 copy-start.21
  448.6 7.1 copy-start.23
  448.6 7.4 copy-start.7
  457.1 811.7 %reduce-scatter.10.cloned.1.call-start = ((), (), s32[]{:S(2)}) async-start(), calls=%async_computation.12 | async-start | bytes 4325376 | tf_op jit(solution)/shard_map/reduce_scatter | solution.py:241
  460.0 808.9 %reduce-scatter.12.cloned.1.call-start = ((), (), s32[]{:S(2)}) async-start(), calls=%async_computation.13 | async-start | bytes 11354112
  479.8 789.0 %reduce-scatter.8.cloned.1.call-start = ((), (), s32[]{:S(2)}) async-start(), calls=%async_computation.11 | async-start | bytes 12976128 | tf_op jit(solution)/shard_map/reduce_scatter | solution.py:240
  521.6 33.4 %copy-start.6 = (bf16[128,16,64]{0,2,1:T(8,128)(2,1)S(1)}, bf16[128,16,64]{0,2,1:T(8,128)(2,1)}, u32[]{:S(2)}) copy-start(bf16[128,16,64]{0,2,1:T(8,128)(2,1)} %get-tuple-element.919) | copy-start | bytes 786436
  555.0 65.3 %copy-start.28 = (f32[128,64]{0,1:T(8,128)S(1)}, f32[128,64]{0,1:T(8,128)}, u32[]{:S(2)}) copy-start(f32[128,64]{0,1:T(8,128)} %copy-done.27) | copy-start | bytes 98308
  640.0 552.9 %copy-start.3 = (f32[128,5248]{1,0:T(8,128)S(1)}, f32[128,5248]{1,0:T(8,128)}, u32[]{:S(2)}) copy-start(f32[128,5248]{1,0:T(8,128)} %fusion.87) | copy-start | bytes 8060932
  1189.1 16.7 %collective-permute-start = (f32[124,1024]{1,0:T(8,128)}, f32[124,1024]{1,0:T(8,128)}, u32[]{:S(2)}, u32[]{:S(2)}) collective-permute-start(f32[124,1024]{1,0:T(8,128)} %slice.67), channel_id=1, source_target_pairs={{0,1},{1,2},{2,3},{3,4},{4,5},{5,6},{6,7},{7,8},{8,9},{9,10},{10,1... | collective-permute-start | bytes 1523720
  1197.4 12.5 copy-start.11
  1197.4 12.5 copy-start.13
  1197.4 12.5 copy-start.15
  1209.9 57.9 %copy-start.9 = (f32[128,1024]{1,0:T(8,128)S(1)}, f32[128,1024]{1,0:T(8,128)}, u32[]{:S(2)}) copy-start(f32[128,1024]{1,0:T(8,128)} %copy-done.8) | copy-start | bytes 1572868
  (26 other events, 55.5 us)
Sparse Core Ops, SparseCore 0:
  9.5 80.5 all-gather.8
  103.4 50.4 all-gather.10
  156.1 48.8 all-gather.12
  206.4 31.5 all-gather.14
  239.4 132.3 all-gather.16
  373.2 70.0 all-gather.18
  445.4 50.5 all-gather.20
  498.1 49.5 all-gather.22
  550.6 139.3 reduce-scatter.9
  696.4 204.9 reduce-scatter.11
  908.0 196.3 reduce-scatter.7
where the time goes:
time: 1280 us
  blocking collectives  637 us (50%)
  waiting for transfers between devices  373 us (29%)
  matrix products  152 us (12%)
  local copies, waits for them, and re-layouts  82 us (6%)
  between operations  15 us (1%)
    unnamed x2, blocking collectives  600 us
    all_gather x1, waiting for transfers between devices, per_device(): lax.all_gather(in_weight, 'fsdp', axis=0, tiled=True)  128 us
    all_gather x1, waiting for transfers between devices, per_device(): lax.all_gather(qkv_weight, 'fsdp', axis=0, tiled=True)  80.5 us
    all_gather x1, waiting for transfers between devices, per_device(): lax.all_gather(down_weight, 'fsdp', axis=0, tiled=True)  62.2 us
    all_gather x1, waiting for transfers between devices, per_device(): key_piece = lax.all_gather(key_send, 'ctx', axis=0, tiled=True)  47.2 us
    all_gather x1, waiting for transfers between devices, per_device(): value_piece = lax.all_gather(value_send, 'ctx', axis=0, tiled=True)  44.6 us
    unnamed x92, local copies, waits for them, and re-layouts  36 us
    dot_general x4, matrix products, rows_contract(): lax.dot_general(left, right, (((0,), (0,)), ((), ())), preferred_element_...  26 us
  transfers between devices with their start and end apart: 12, of which 6 were waited for; matrix products, arithmetic and copies ran while one was open for 61% of the time, Pallas kernels for 0%

commit v1 on v0

--- a/solution.py
+++ b/solution.py
@@ -9,6 +9,28 @@
 ROPE_BASE = 160000.0
 
 
+def divide_the_ranges(point, axis_k):
+    taken_in = list(point.shape[1:])
+    taken_in[axis_k] *= point.shape[0]
+    arr_next = jnp.moveaxis(point, 0, axis_k).reshape(taken_in)
+    return arr_next
+
+
+def press_slots_here(z, along_axis):
+    tall, answer = (jax.lax.axis_size(along_axis), jax.lax.axis_index(along_axis))
+    ready, step_out = (z[None], 1)
+    while step_out < tall:
+        row_out = jax.lax.ppermute(
+            ready, along_axis, perm=tuple(((u, u ^ step_out) for u in range(tall)))
+        )
+        value_now = answer & step_out == 0
+        ready = jnp.concatenate(
+            [jnp.where(value_now, ready, row_out), jnp.where(value_now, row_out, ready)]
+        )
+        step_out *= 2
+    return ready
+
+
 def normalize(tensor):
     centred = tensor - jnp.mean(tensor, axis=-1, keepdims=True)
     inv_std = lax.rsqrt(jnp.mean(centred * centred, axis=-1, keepdims=True) + EPSILON)
@@ -67,10 +89,15 @@
 def per_device(
     tokens, cotangent, gain_attn, gain_mlp, qkv_weight, out_weight, in_weight, down_weight
 ):
+
+    def side_place(my_data, work_x, dim_i):
+        even = divide_the_ranges(press_slots_here(my_data, work_x), dim_i)
+        return even
+
     f32 = jnp.float32
     bf16 = jnp.bfloat16
     qkv_full, out_full, in_full, down_full = (
-        lax.all_gather(qkv_weight, "fsdp", axis=0, tiled=True),
+        side_place(qkv_weight, work_x="fsdp", dim_i=0),
         lax.all_gather(out_weight, "fsdp", axis=0, tiled=True),
         lax.all_gather(in_weight, "fsdp", axis=0, tiled=True),
         lax.all_gather(down_weight, "fsdp", axis=0, tiled=True),

time: 1280 us -> 1270 us (level)
  waiting for transfers between devices: 373 us -> 357 us
    all_gather x1 -> x0, waiting for transfers between devices: 80.5 us -> none  [per_device(): lax.all_gather(qkv_weight, 'fsdp', axis=0, tiled=True)]
    ppermute x0 -> x1, waiting for transfers between devices: none -> 64.2 us  [press_slots_here(): jax.lax.ppermute(ready, along_axis, perm=tuple(((u, u ^ step_out) for u i...]
    unnamed x92 -> x94, local copies, waits for them, and re-layouts: 36 us -> 36.4 us
  transfers between devices with their start and end apart: 12 -> 12, of which waited for: 6 -> 6; matrix products, arithmetic and copies ran while one was open for 61% -> 62% of each run, Pallas kernels for 0% -> 0%
where the time goes in v1:
time: 1270 us; the launch traced here: 1260 us
  blocking collectives  637 us (50%)
  waiting for transfers between devices  357 us (28%)
  matrix products  149 us (12%)
  local copies, waits for them, and re-layouts  84.2 us (7%)
  other arithmetic  15.8 us (1%)
  between operations  15.3 us (1%)
    unnamed x2, blocking collectives  600 us
    all_gather x1, waiting for transfers between devices, per_device(): lax.all_gather(in_weight, 'fsdp', axis=0, tiled=True)  128 us
    ppermute x1, waiting for transfers between devices, press_slots_here(): jax.lax.ppermute(ready, along_axis, perm=tuple(((u, u ^ step_out) for u i...  64.2 us
    all_gather x1, waiting for transfers between devices, per_device(): lax.all_gather(down_weight, 'fsdp', axis=0, tiled=True)  62.2 us
    all_gather x1, waiting for transfers between devices, per_device(): key_piece = lax.all_gather(key_send, 'ctx', axis=0, tiled=True)  47.4 us
    all_gather x1, waiting for transfers between devices, per_device(): value_piece = lax.all_gather(value_send, 'ctx', axis=0, tiled=True)  44.6 us
    unnamed x94, local copies, waits for them, and re-layouts  36.4 us
    dot_general x4, matrix products, rows_contract(): lax.dot_general(left, right, (((0,), (0,)), ((), ())), preferred_element_...  26 us
  transfers between devices with their start and end apart: 12, of which 6 were waited for; matrix products, arithmetic and copies ran while one was open for 62% of the time, Pallas kernels for 0%

profile of v1, /device:TPU:14, one launch (start us, length us, event | category | flops | bytes accessed | tf_op | source)
XLA Modules:
  0.0 1263.8 jit_solution(2152691232269389803)
XLA Ops:
  13.1 64.2 %collective-permute-done = bf16[1,1536,1024]{2,1,0:T(8,128)(2,1)S(1)} collective-permute-done((bf16[1,1536,1024]{2,1,0:T(8,128)(2,1)}, bf16[1,1536,1024]{2,1,0:T(8,128)(2,1)S(1)}, u32[]{:S(2)}, u32[]{:S(2)}) %collective-permute-start) | collective-permute-done | bytes 3145760 | tf_op jit(solution)/shard_map/ppermute | solution.py:23
  94.4 47.4 %all-gather.8.cloned.1.call-done = bf16[2048,1024]{1,0:T(8,128)(2,1)} async-done(((bf16[128,1024]{1,0:T(8,128)(2,1)}), bf16[2048,1024]{1,0:T(8,128)(2,1)}) %all-gather.8.cloned.1.call-update) | async-done | bytes 4194320 | tf_op jit(solution)/shard_map/all_gather | solution.py:131
  141.8 6.5 copy.63
  148.3 44.6 %all-gather.10.cloned.1.call-done = bf16[2048,1024]{1,0:T(8,128)(2,1)} async-done(((bf16[128,1024]{1,0:T(8,128)(2,1)}), bf16[2048,1024]{1,0:T(8,128)(2,1)}) %all-gather.10.cloned.1.call-update) | async-done | bytes 4194320 | tf_op jit(solution)/shard_map/all_gather | solution.py:132
  192.9 6.5 copy.64
  199.4 29.9 %while.48 = (s32[]{:T(128)}, f32[128,16,64]{0,2,1:T(8,128)S(1)}, f32[16,128]{1,0:T(8,128)S(1)}, f32[16,128]{1,0:T(8,128)S(1)}, bf16[2048,1024]{0,1:T(8,128)(2,1)...) while((s32[]{:T(128)}, f32[128,16,64]{0,2,1:T(8,128)S(1)}, ...), condition=%wide.region_5.6_spmd.clone, body=%wide.region_2.5_spmd.clone.sunk | while | flops 554053632 | bytes 72745168 | solution.py:156
  202.5 4.8 bitcast_reduce_fusion.2
  207.3 5.3 fusion.158
  217.2 4.8 bitcast_reduce_fusion.2
  222.0 5.3 fusion.158
  232.2 127.7 %all-gather.14.cloned.1.call-done = bf16[5248,1024]{1,0:T(8,128)(2,1)} async-done(((bf16[2624,1024]{1,0:T(8,128)(2,1)}), bf16[5248,1024]{1,0:T(8,128)(2,1)}) %all-gather.14.cloned.1.call-update) | async-done | bytes 10747920 | tf_op jit(solution)/shard_map/all_gather | solution.py:102
  359.9 9.3 fusion.97
  369.1 62.2 %all-gather.16.cloned.1.call-done = bf16[1024,2624]{0,1:T(8,128)(2,1)} async-done(((bf16[512,2624]{0,1:T(8,128)(2,1)}), bf16[1024,2624]{0,1:T(8,128)(2,1)}) %all-gather.16.cloned.1.call-update) | async-done | bytes 5373968 | tf_op jit(solution)/shard_map/all_gather | solution.py:103
  431.3 5.3 fusion.48
  436.6 7.1 multiply_reduce_fusion
  448.1 7.7 convolution_bitcast_fusion
  455.7 12.1 copy.78
  471.1 15.4 %all_gather.35 = f32[2048,16]{0,1:T(8,128)S(1)} all-gather(f32[128,16]{0,1:T(8,128)S(1)} %bitcast.227), channel_id=1, replica_groups=mesh['ctx'=16,'fsdp'=2] {'ctx'}, dimensions={0}, use_global_device_ids=true | all-gather | bytes 139264 | tf_op jit(solution)/shard_map/all_gather | solution.py:213
  487.5 22.2 %all_gather.37 = f32[2048,16]{0,1:T(8,128)S(1)} all-gather(f32[128,16]{0,1:T(8,128)S(1)} %multiply_reduce_fusion.1), channel_id=1, replica_groups=mesh['ctx'=16,'fsdp'=2] {'ctx'}, dimensions={0}, use_global_device_ids=true | all-gather | bytes 139264 | tf_op jit(solution)/shard_map/all_gather | solution.py:214
  509.7 33.4 %while.49 = (s32[]{:T(128)}, f32[128,16,64]{0,2,1:T(8,128)}, bf16[2048,1024]{0,1:T(8,128)(2,1)}, bf16[128,16,64]{0,2,1:T(8,128)(2,1)S(1)}, f32[16,128]{1,0:T(8,1...) while((s32[]{:T(128)}, f32[128,16,64]{0,2,1:T(8,128)}, ...), condition=%wide.region_12.13_spmd.clone, body=%wide.region_11.12_spmd.clone.sunk | while | flops 816185344 | bytes 33079508 | solution.py:208
  518.4 8.1 fusion.167
  535.1 8.0 fusion.167
  543.1 65.2 %while.50 = (s32[]{:T(128)}, f32[128,16,64]{0,2,1:T(8,128)}, f32[128,16,64]{0,2,1:T(8,128)S(1)}, bf16[2048,1024]{1,0:T(8,128)(2,1)}, bf16[128,16,64]{0,2,1:T(8,1...) while((s32[]{:T(128)}, f32[128,16,64]{0,2,1:T(8,128)}, ...), condition=%wide.region_14.15_spmd.clone, body=%wide.region_13.14_spmd.clone.sunk | while | flops 1091174400 | bytes 53412036 | solution.py:249
  559.5 10.8 fusion.176
  570.3 5.5 fusion.177
  592.0 10.8 fusion.176
  602.8 5.5 fusion.177
  611.0 6.4 fusion.72
  618.9 9.2 fusion.50
  628.1 546.9 %fusion = f32[168,1024]{1,0:T(8,128)} fusion(f32[5248,1024]{1,0:T(8,128)} %fusion.50), kind=kCustom, calls=%all-reduce-scatter | all-reduce-scatter fusion | flops 5505025 | bytes 22183936
  1185.2 8.1 collective-permute-done.1
  1201.4 52.8 %all-reduce.4 = (f32[1024]{0:T(1024)S(1)}, f32[1024]{0:T(1024)S(1)}) all-reduce(f32[1024]{0:T(1024)S(1)} %get-tuple-element.613, f32[1024]{0:T(1024)S(1)} %copy-done.44), channel_id=6, replica_groups=mesh['ctx'=16,'fsdp'=2] {'ctx','fsdp'}, use_global_device_ids=true, to_apply=%region_22.23.clone | all-reduce | flops 2048 | bytes 16384
  (203 shorter events, 117.6 us)
Async XLA Ops:
  7.2 134.6 %all-gather.8.cloned.1.call-start = ((), (), s32[]{:S(2)}) async-start(), calls=%async_computation.3 | async-start | bytes 4456448 | tf_op jit(solution)/shard_map/all_gather | solution.py:131
  7.2 70.1 %collective-permute-start = (bf16[1,1536,1024]{2,1,0:T(8,128)(2,1)}, bf16[1,1536,1024]{2,1,0:T(8,128)(2,1)S(1)}, u32[]{:S(2)}, u32[]{:S(2)}) collective-permute-start(bf16[1,1536,1024]{2,1,0:T(8,128)(2,1)} %bitcast.211), channel_id=1, source_target_pairs={{0,1},{1,0},{2,3},{3,2},{4,5},{5,4},{6,7},{7,6},{8,9},{9,8},{10,11... | collective-permute-start | bytes 9437192 | tf_op jit(solution)/shard_map/ppermute | solution.py:23
  8.0 77.4 %copy-start.26 = (f32[128,64]{0,1:T(8,128)}, f32[128,64]{0,1:T(8,128)S(1)}, u32[]{:S(2)}) copy-start(f32[128,64]{0,1:T(8,128)S(1)} %get-tuple-element.706) | copy-start | bytes 98308
  8.0 77.4 %copy-start.28 = (f32[128,64]{0,1:T(8,128)}, f32[128,64]{0,1:T(8,128)S(1)}, u32[]{:S(2)}) copy-start(f32[128,64]{0,1:T(8,128)S(1)} %get-tuple-element.705) | copy-start | bytes 98308
  11.9 68.3 %copy-start.36 = (f32[128]{0:T(128)}, f32[128]{0:T(128)S(1)}, u32[]{:S(2)}) copy-start(f32[128]{0:T(128)S(1)} %broadcast_multiply_fusion.8) | copy-start | bytes 1540
  13.1 67.1 %copy-start.38 = (f32[128]{0:T(128)}, f32[128]{0:T(128)S(1)}, u32[]{:S(2)}) copy-start(f32[128]{0:T(128)S(1)} %add_rsqrt_fusion.1) | copy-start | bytes 1540
  91.1 101.8 %all-gather.10.cloned.1.call-start = ((), (), s32[]{:S(2)}) async-start(), calls=%async_computation.4 | async-start | bytes 4456448 | tf_op jit(solution)/shard_map/all_gather | solution.py:132
  91.9 137.5 %all-gather.12.cloned.1.call-start = ((), (), s32[]{:S(2)}) async-start(), calls=%async_computation.5 | async-start | bytes 3145728 | tf_op jit(solution)/shard_map/all_gather | solution.py:101
  92.6 267.3 %all-gather.14.cloned.1.call-start = ((), (), s32[]{:S(2)}) async-start(), calls=%async_computation.6 | async-start | bytes 16121856 | tf_op jit(solution)/shard_map/all_gather | solution.py:102
  93.2 338.1 %all-gather.16.cloned.1.call-start = ((), (), s32[]{:S(2)}) async-start(), calls=%async_computation.7 | async-start | bytes 8060928 | tf_op jit(solution)/shard_map/all_gather | solution.py:103
  93.8 449.3 %all-gather.18.cloned.1.call-start = ((), (), s32[]{:S(2)}) async-start(), calls=%async_computation.8 | async-start | bytes 4456448 | tf_op jit(solution)/shard_map/all_gather | solution.py:211
  94.3 448.7 %all-gather.20.cloned.1.call-start = ((), (), s32[]{:S(2)}) async-start(), calls=%async_computation.9 | async-start | bytes 4456448 | tf_op jit(solution)/shard_map/all_gather | solution.py:212
  207.3 5.8 copy-start
  229.3 130.6 %copy-start.32 = (f32[1024]{0:T(1024)S(1)}, f32[1024]{0:T(1024)}, u32[]{:S(2)}) copy-start(f32[1024]{0:T(1024)} %param.17) | copy-start | bytes 12292
  231.9 211.8 %copy-start.2 = (f32[128,1024]{1,0:T(8,128)}, f32[128,1024]{1,0:T(8,128)S(1)}, u32[]{:S(2)}) copy-start(f32[128,1024]{1,0:T(8,128)S(1)} %get-tuple-element.708) | copy-start | bytes 1572868
  231.9 211.8 %copy-start.40 = (f32[128]{0:T(128)}, f32[128]{0:T(128)S(1)}, u32[]{:S(2)}) copy-start(f32[128]{0:T(128)S(1)} %broadcast_multiply_fusion.7) | copy-start | bytes 1540
  232.2 211.6 %copy-start.42 = (f32[128]{0:T(128)}, f32[128]{0:T(128)S(1)}, u32[]{:S(2)}) copy-start(f32[128]{0:T(128)S(1)} %add_rsqrt_fusion) | copy-start | bytes 1540
  232.2 199.1 %copy-start.21 = (bf16[1,128,1024]{2,1,0:T(8,128)(2,1)S(1)}, bf16[1,128,1024]{2,1,0:T(8,128)(2,1)}, u32[]{:S(2)}) copy-start(bf16[1,128,1024]{2,1,0:T(8,128)(2,1)} %param.15) | copy-start | bytes 786436
  436.6 7.1 copy-start.22
  436.6 7.1 copy-start.24
  436.6 7.4 copy-start.8
  445.2 811.3 %reduce-scatter.10.cloned.1.call-start = ((), (), s32[]{:S(2)}) async-start(), calls=%async_computation.11 | async-start | bytes 4325376 | tf_op jit(solution)/shard_map/reduce_scatter | solution.py:268
  448.0 808.5 %reduce-scatter.12.cloned.1.call-start = ((), (), s32[]{:S(2)}) async-start(), calls=%async_computation.12 | async-start | bytes 11354112
  467.9 788.7 %reduce-scatter.8.cloned.1.call-start = ((), (), s32[]{:S(2)}) async-start(), calls=%async_computation.10 | async-start | bytes 12976128 | tf_op jit(solution)/shard_map/reduce_scatter | solution.py:267
  509.7 33.4 %copy-start.7 = (bf16[128,16,64]{0,2,1:T(8,128)(2,1)S(1)}, bf16[128,16,64]{0,2,1:T(8,128)(2,1)}, u32[]{:S(2)}) copy-start(bf16[128,16,64]{0,2,1:T(8,128)(2,1)} %get-tuple-element.921) | copy-start | bytes 786436
  543.1 65.3 %copy-start.29 = (f32[128,64]{0,1:T(8,128)S(1)}, f32[128,64]{0,1:T(8,128)}, u32[]{:S(2)}) copy-start(f32[128,64]{0,1:T(8,128)} %copy-done.28) | copy-start | bytes 98308
  628.1 552.6 %copy-start.4 = (f32[128,5248]{1,0:T(8,128)S(1)}, f32[128,5248]{1,0:T(8,128)}, u32[]{:S(2)}) copy-start(f32[128,5248]{1,0:T(8,128)} %fusion.97) | copy-start | bytes 8060932
  1176.9 16.4 %collective-permute-start.1 = (f32[124,1024]{1,0:T(8,128)}, f32[124,1024]{1,0:T(8,128)}, u32[]{:S(2)}, u32[]{:S(2)}) collective-permute-start(f32[124,1024]{1,0:T(8,128)} %slice.67), channel_id=1, source_target_pairs={{0,1},{1,2},{2,3},{3,4},{4,5},{5,6},{6,7},{7,8},{8,9},{9,10},{10,1... | collective-permute-start | bytes 1523720
  1185.2 12.2 copy-start.12
  1185.2 12.2 copy-start.14
  1185.2 12.2 copy-start.16
  1197.4 58.0 %copy-start.10 = (f32[128,1024]{1,0:T(8,128)S(1)}, f32[128,1024]{1,0:T(8,128)}, u32[]{:S(2)}) copy-start(f32[128,1024]{1,0:T(8,128)} %copy-done.9) | copy-start | bytes 1572868
  (27 other events, 52.2 us)
Sparse Core Ops, SparseCore 0:
  91.2 50.5 all-gather.7
  144.0 48.8 all-gather.9
  194.5 31.5 all-gather.11
  227.5 132.3 all-gather.13
  361.3 70.0 all-gather.15
  433.3 50.4 all-gather.17
  486.0 49.4 all-gather.19
  538.4 139.8 reduce-scatter.9
  684.9 205.1 reduce-scatter.11
  896.5 194.0 reduce-scatter.7
